TPU v7x, 32 devices: a whole 2x2x4 slice. The times are simulated.
32 devices in a mesh: member: 2 (over x), lat: 16 (over z, y, core).
Axes of the slice: x: 2, y: 2, z: 4, core: 2. Of those that a mesh axis runs over, the one named last changes fastest.
Arguments:
- field: bfloat16 [192, 1440, 256], P(('member', 'lat')), parts along dimension 0, may hold values from -3000 to 3000
- gain: float32 [256], replicated, may hold values from 0.1 to 1.9
- slot_wave: int32 [96], replicated, may hold values from 0 to 96, as said below
- legendre: bfloat16 [96, 96, 96], P('lat'), may hold values from -0.625 to 0.625
- mixing: bfloat16 [96, 2, 256, 256], P('lat'), may hold values from -0.25 to 0.25
Outputs:
- result: bfloat16 [192, 1440, 256], P(('member', 'lat')), parts along dimension 0
There are 2 independent parts, one for each index of `member`. A program takes and returns all parts, laid end to end along the dimension named above; an argument that names none is the same for every part. Nothing has to cross between parts.
Inputs may be any that keep to these rules, and one draw needn't show every extreme that they name: `slot_wave`: each wavenumber 0 to 95 stands in exactly one slot and every other slot holds 96; slots 2k and 2k+1 of one lat index hold wavenumbers adding up to (4k+2)16 - 1 where both are below 96.
All inputs are finite; a program needn't handle non-finite values.
Results may differ from a plain program's by a relative error of at most 0.0085.
Values may be sent and summed in bfloat16 or wider, within the bound.
A program may use at most 64 MiB of HBM per device.

v0:
```python
import math

import jax
import jax.numpy as jnp
from jax import lax
from jax.sharding import PartitionSpec as P


def phase_tables(waves, width):
    points = jnp.arange(width, dtype=jnp.int32)
    phase = (waves[:, None] * points[None, :] % width).astype(jnp.float32) * (2.0 * math.pi / width)
    return (jnp.cos(phase), jnp.sin(phase))


def block_weight(mixing):
    real_part = mixing[:, 0]
    imag_part = mixing[:, 1]
    upper = jnp.concatenate([real_part, imag_part], axis=2)
    lower = jnp.concatenate([-imag_part, real_part], axis=2)
    return jnp.concatenate([upper, lower], axis=1)


def per_device(field, gain, slot_wave, legendre, mixing):
    lat_count = lax.axis_size("lat")
    lat_dev, width, chans = field.shape
    slot_dev, degs, nlat = legendre.shape
    count = float(lat_dev * lat_count * width)
    values = field.astype(jnp.float32)
    local_sum = jnp.sum(values, axis=(0, 1))
    local_sq = jnp.sum(values * values, axis=(0, 1))
    total, squares = lax.psum((local_sum, local_sq), "lat")
    mean = total / count
    var = squares / count - mean * mean
    normed = ((values - mean) * (gain / jnp.sqrt(var + 1e-05))).astype(jnp.bfloat16)
    cosine, sine = phase_tables(slot_wave, width)
    forward = jnp.stack([cosine, -sine]).astype(jnp.bfloat16).reshape(2, lat_count, slot_dev, width)
    weight_m = jnp.where(slot_wave == 0, 1.0, 2.0).astype(jnp.float32)[:, None]
    inverse = jnp.stack([weight_m * cosine, -weight_m * sine]).astype(jnp.bfloat16)
    inv_root = 1.0 / math.sqrt(width)
    spectrum = (
        jnp.einsum("anc,rdjn->dajrc", normed, forward, preferred_element_type=jnp.float32)
        * inv_root
    )
    spectrum = spectrum.astype(jnp.bfloat16).reshape(lat_count, lat_dev, slot_dev, 2 * chans)
    arrived = lax.all_to_all(spectrum, "lat", split_axis=0, concat_axis=1, tiled=True)[0]
    mine = lax.dynamic_slice_in_dim(slot_wave, lax.axis_index("lat") * slot_dev, slot_dev, 0)
    big = block_weight(mixing)
    lat_scale = math.sqrt(nlat / degs)
    degrees = jnp.arange(degs, dtype=jnp.int32)
    coef = jnp.einsum("jlt,tjc->jlc", legendre, arrived, preferred_element_type=jnp.float32)
    coef = jnp.where((degrees[None, :] >= mine[:, None])[:, :, None], coef, 0.0).astype(
        jnp.bfloat16
    )
    mixed = jnp.einsum("jlc,jcd->jld", coef, big, preferred_element_type=jnp.float32).astype(
        jnp.bfloat16
    )
    back = (
        jnp.einsum("jlt,jld->tjd", legendre, mixed, preferred_element_type=jnp.float32) * lat_scale
    )
    back = back.astype(jnp.bfloat16)
    back = back.reshape(lat_count, lat_dev, slot_dev, 2 * chans)
    returned = lax.all_to_all(back, "lat", split_axis=0, concat_axis=2, tiled=True)[0]
    returned = returned.reshape(lat_dev, slot_dev * lat_count, 2, chans)
    filtered = (
        jnp.einsum("akrc,rkn->anc", returned, inverse, preferred_element_type=jnp.float32)
        * inv_root
    )
    return (normed.astype(jnp.float32) + filtered).astype(jnp.bfloat16)


def solution(mesh):
    return jax.shard_map(
        per_device,
        mesh=mesh,
        in_specs=(
            P(("member", "lat"), None, None),
            P(),
            P(),
            P("lat", None, None),
            P("lat", None, None, None),
        ),
        out_specs=P(("member", "lat"), None, None),
        check_vma=False,
    )
```

profile of v0, /device:TPU:0, one launch (start us, length us, event | category | flops | bytes accessed | tf_op | source)
XLA Modules:
  0.0 103.8 jit_solution(11740767256744801090)
XLA Ops:
  0.0 0.0 copy-start
  0.0 0.0 copy-start.2
  0.0 0.0 copy-start.3
  0.0 3.5 %convert_reduce_fusion = (f32[256]{0:T(256)S(1)}, f32[256]{0:T(256)S(1)}) fusion(bf16[6,1440,256]{2,1,0:T(8,128)(2,1)} %param.5), kind=kLoop, calls=%fused_computation.2 | loop fusion | flops 8846848 | bytes 4425728 | tf_op jit(solution)/shard_map/reduce_sum | solution.py:29
  3.5 0.0 copy-done.2
  3.5 0.1 mul.154
  3.6 0.1 copy.23
  3.7 2.8 %cosine_convert_fusion = (bf16[1,16,6,1440]{3,1,2,0:T(8,128)(2,1)S(1)}, bf16[1,16,6,1440]{3,1,2,0:T(8,128)(2,1)S(1)}) fusion(s32[16,6]{0,1:T(8,128)S(1)} %copy.23), kind=kLoop, calls=%fused_computation.44 | loop fusion | flops 1658880 | bytes 553344 | tf_op jit(solution)/shard_map/convert
  6.5 35.0 %all-reduce = (f32[256]{0:T(256)S(1)}, f32[256]{0:T(256)S(1)}) all-reduce(f32[256]{0:T(256)S(1)} %get-tuple-element.6, f32[256]{0:T(256)S(1)} %get-tuple-element.5), channel_id=1, replica_groups=mesh['member'=2,'lat'=16] {'lat'}, use_global_device_ids=true, to_apply=%region_3.0 | all-reduce | flops 512 | bytes 4096 | tf_op jit(solution)/shard_map/psum | solution.py:31
  41.5 0.0 copy-done.3
  41.5 3.6 %fusion.26 = bf16[16,6,6,2,256]{4,0,1,2,3:T(8,128)(2,1)S(1)} fusion(f32[256]{0:T(256)S(1)} %get-tuple-element.14, f32[256]{0:T(256)S(1)} %get-tuple-element.13, bf16[6,1440,256]{2,1,0:T(8,128)(2,1)} %param.5, bf16[1,16,6,1440]{3,1,2,0:T(8,128)(2,1)S(1)} %get-tuple-element.12, bf16[1,16,6,1440]{3,1,2,0:T(8,128)(2,1)S(1)} %get-tuple-element.11), kind=kOutput, calls=%fused_computation.26 | convolution fusion | flops 859889664 | bytes 5568512 | tf_op jit(solution)/shard_map/anc,rdjn->dajrc/dot_general | solution.py:41
  45.1 0.0 copy-start.1
  45.1 0.6 copy.37
  45.8 1.3 %reshape.223 = bf16[16,6,6,512]{3,2,1,0:T(8,128)(2,1)} reshape(bf16[16,6,6,2,256]{4,3,2,1,0:T(2,128)(2,1)S(1)} %copy.37) | data formatting | bytes 1179648 | tf_op jit(solution)/shard_map/reshape | solution.py:44
  47.0 3.6 %all-to-all-start = ((bf16[16,6,6,512]{3,2,1,0:T(8,128)(2,1)}), bf16[16,6,6,512]{3,2,1,0:T(8,128)(2,1)S(1)}, u32[]{:S(2)}, u32[]{:S(2)}) async-start(bf16[16,6,6,512]{3,2,1,0:T(8,128)(2,1)} %reshape.223), calls=%async_computation | async-start | bytes 1572864 | tf_op jit(solution)/shard_map/all_to_all | solution.py:45
  50.7 0.1 dynamic_slice.3
  50.7 0.1 iota_compare_fusion
  50.8 0.0 copy-done.1
  50.8 0.1 fusion.52
  50.9 1.3 %slice_bitcast_fusion = (bf16[6,256,256]{2,1,0:T(8,128)(2,1)}, bf16[6,256,256]{2,1,0:T(8,128)(2,1)}) fusion(bf16[6,2,256,256]{3,2,1,0:T(8,128)(2,1)S(1)} %copy-done.1), kind=kLoop, calls=%fused_computation.29 | loop fusion | bytes 3145728 | tf_op jit(solution)/shard_map/squeeze | solution.py:17
  52.1 17.2 %all-to-all-done = bf16[16,6,6,512]{3,2,1,0:T(8,128)(2,1)S(1)} async-done(((bf16[16,6,6,512]{3,2,1,0:T(8,128)(2,1)}), bf16[16,6,6,512]{3,2,1,0:T(8,128)(2,1)S(1)}, u32[]{:S(2)}, u32[]{:S(2)}) %all-to-all-start) | async-done | bytes 589856 | tf_op jit(solution)/shard_map/all_to_all | solution.py:45
  69.3 0.0 copy-done
  69.3 0.4 fusion.18
  69.7 2.4 %fusion.25 = bf16[96,6,512]{2,0,1:T(8,128)(2,1)S(1)} fusion(bf16[6,96,96]{2,1,0:T(8,128)(2,1)S(1)} %copy-done, bf16[6,512,96]{1,2,0:T(8,128)(2,1)S(1)} %fusion.18, bf16[6,256,256]{2,1,0:T(8,128)(2,1)} %get-tuple-element.10, bf16[6,256,256]{2,1,0:T(8,128)(2,1)S(1)} %fusion.52, bf16[6,256,256]{2,1,0:T(8,128)(2,1)} %get-tuple-element.9), kind=kOutput, calls=%fused_computation.25 | convolution fusion | flops 371785728 | bytes 3649536 | tf_op jit(solution)/shard_map/jlt,jld->tjd/dot_general | solution.py:58
  72.1 0.2 reshape.218
  72.3 1.0 copy.30
  73.3 5.3 %all-to-all-start.1 = ((bf16[16,6,6,512]{3,1,2,0:T(8,128)(2,1)}), bf16[16,6,6,512]{3,1,2,0:T(8,128)(2,1)S(1)}, u32[]{:S(2)}, u32[]{:S(2)}) async-start(bf16[16,6,6,512]{3,1,2,0:T(8,128)(2,1)} %copy.30), calls=%async_computation.1 | async-start | bytes 1572864 | tf_op jit(solution)/shard_map/all_to_all | solution.py:62
  78.6 2.9 %multiply_convert_fusion.1 = (bf16[1,96,1440]{2,1,0:T(8,128)(2,1)S(1)}, bf16[1,96,1440]{2,1,0:T(8,128)(2,1)S(1)}) fusion(s32[96]{0:T(128)S(1)} %copy-done.2, f32[96]{0:T(128)S(1)} %get-tuple-element.17, f32[96]{0:T(128)S(1)} %get-tuple-element.18), kind=kLoop, calls=%fused_computation.49 | loop fusion | flops 1797120 | bytes 554112 | tf_op jit(solution)/shard_map/convert.2
  81.5 15.8 %all-to-all-done.1 = bf16[16,6,6,512]{3,1,2,0:T(8,128)(2,1)S(1)} async-done(((bf16[16,6,6,512]{3,1,2,0:T(8,128)(2,1)}), bf16[16,6,6,512]{3,1,2,0:T(8,128)(2,1)S(1)}, u32[]{:S(2)}, u32[]{:S(2)}) %all-to-all-start.1) | async-done | bytes 589856 | tf_op jit(solution)/shard_map/all_to_all | solution.py:62
  97.3 0.3 reshape.224
  97.6 6.2 %fusion.3 = bf16[6,1440,256]{2,1,0:T(8,128)(2,1)} fusion(f32[256]{0:T(256)S(1)} %get-tuple-element.14, f32[256]{0:T(256)S(1)} %get-tuple-element.13, bf16[6,1440,256]{2,1,0:T(8,128)(2,1)} %param.5, bf16[1,96,1440]{2,1,0:T(8,128)(2,1)S(1)} %get-tuple-element.16, bf16[1,96,1440]{2,1,0:T(8,128)(2,1)S(1)} %get-tuple-element.15, ...), kind=kOutput, calls=%fused_computation.7 | convolution fusion | flops 868147200 | bytes 9992192 | tf_op jit(solution)/shard_map/akrc,rkn->anc/dot_general | solution.py:65
  (2 shorter events, 0.0 us)
Async XLA Ops:
  0.0 69.3 %copy-start = (bf16[6,96,96]{2,1,0:T(8,128)(2,1)S(1)}, bf16[6,96,96]{2,1,0:T(8,128)(2,1)}, u32[]{:S(2)}) copy-start(bf16[6,96,96]{2,1,0:T(8,128)(2,1)} %param.8) | copy-start | bytes 331780
  0.0 3.5 %copy-start.2 = (s32[96]{0:T(128)S(1)}, s32[96]{0:T(128)}, u32[]{:S(2)}) copy-start(s32[96]{0:T(128)} %param.7) | copy-start | bytes 1156
  0.0 41.5 %copy-start.3 = (f32[256]{0:T(256)S(1)}, f32[256]{0:T(256)}, u32[]{:S(2)}) copy-start(f32[256]{0:T(256)} %param.6) | copy-start | bytes 3076
  45.1 5.7 %copy-start.1 = (bf16[6,2,256,256]{3,2,1,0:T(8,128)(2,1)S(1)}, bf16[6,2,256,256]{3,2,1,0:T(8,128)(2,1)}, u32[]{:S(2)}) copy-start(bf16[6,2,256,256]{3,2,1,0:T(8,128)(2,1)} %param.9) | copy-start | bytes 4718596
  47.0 22.3 %all-to-all-start = ((bf16[16,6,6,512]{3,2,1,0:T(8,128)(2,1)}), bf16[16,6,6,512]{3,2,1,0:T(8,128)(2,1)S(1)}, u32[]{:S(2)}, u32[]{:S(2)}) async-start(bf16[16,6,6,512]{3,2,1,0:T(8,128)(2,1)} %reshape.223), calls=%async_computation | async-start | bytes 1572864 | tf_op jit(solution)/shard_map/all_to_all | solution.py:45
  73.3 24.0 %all-to-all-start.1 = ((bf16[16,6,6,512]{3,1,2,0:T(8,128)(2,1)}), bf16[16,6,6,512]{3,1,2,0:T(8,128)(2,1)S(1)}, u32[]{:S(2)}, u32[]{:S(2)}) async-start(bf16[16,6,6,512]{3,1,2,0:T(8,128)(2,1)} %copy.30), calls=%async_computation.1 | async-start | bytes 1572864 | tf_op jit(solution)/shard_map/all_to_all | solution.py:62
where the time goes:
time: 104 us
  blocking collectives  35 us (34%)
  waiting for transfers between devices  33 us (32%)
  matrix products  12.6 us (12%)
  other arithmetic  9.31 us (9%)
  starting transfers between devices  8.95 us (9%)
  local copies, waits for them, and re-layouts  4.87 us (5%)
    psum x1, blocking collectives, per_device(): total, squares = lax.psum((local_sum, local_sq), 'lat')  35 us
    all_to_all x1, waiting for transfers between devices, per_device(): lax.all_to_all(spectrum, 'lat', split_axis=0, concat_axis=1, tiled=True)[0]  17.2 us
    all_to_all x1, waiting for transfers between devices, per_device(): lax.all_to_all(back, 'lat', split_axis=0, concat_axis=2, tiled=True)[0]  15.8 us
    dot_general x1, matrix products, per_device(): jnp.einsum('akrc,rkn->anc', returned, inverse, preferred_element_type=jnp...  6.16 us
    another operation x2, other arithmetic  5.69 us
    all_to_all x1, starting transfers between devices, per_device(): lax.all_to_all(back, 'lat', split_axis=0, concat_axis=2, tiled=True)[0]  5.33 us
    dot_general x1, matrix products, per_device(): jnp.einsum('anc,rdjn->dajrc', normed, forward, preferred_element_type=jnp...  3.65 us
    all_to_all x1, starting transfers between devices, per_device(): lax.all_to_all(spectrum, 'lat', split_axis=0, concat_axis=1, tiled=True)[0]  3.61 us
  transfers between devices with their start and end apart: 2, of which 2 were waited for; matrix products, arithmetic and copies ran while one was open for 4% of the time, Pallas kernels for 0%

commit v1 on v0

v1 whole, which is shorter than its diff:
```python
import functools
import math

import jax
import jax.numpy as jnp
import numpy as np
from jax import lax
from jax.experimental import pallas as pl
from jax.experimental.pallas import tpu as pltpu
from jax.sharding import PartitionSpec as P

MESH = pl.DeviceIdType.MESH
F32 = jnp.float32
BF16 = jnp.bfloat16


def wave_table(degs, width):
    pad = -(-(degs + 1) // 128) * 128
    waves = np.arange(degs + 1)[:, None]
    phase = (waves * np.arange(width)[None, :] % width) * (2.0 * np.pi / width)
    table = np.zeros((2, pad, width), np.float32)
    table[0, : degs + 1] = np.cos(phase)
    table[1, : degs + 1] = -np.sin(phase)
    return table.reshape(2 * pad, width).astype(BF16), pad


def dot(a, b):
    return jnp.dot(a, b, preferred_element_type=F32)


def partner(me, step, count):
    if count & (count - 1):
        return lax.rem(me + step, count)
    out = 0
    for bit in range(count.bit_length() - 1):
        size = 2**bit
        mine = lax.rem(me // size, 2)
        flip = lax.rem(step // size, 2)
        out = out + size * (mine + flip - 2 * mine * flip)
    return out


def exchange_kernel(
    count,
    pad,
    field_ref, wave_ref, target_ref, gain_ref, table_ref, tsum_ref, tsum_row_ref, legendre_ref, mixing_ref,
    ret_ref, stat_ref,
    field_v, mix_v, select, raw, spec, send, recv, back_send, stat_src, stat_recv, lbig,
    field_sem, mix_sem, stat_sems, fwd_sems, back_sems,
):
    me = lax.axis_index("lat")
    lat_dev, width, chans = field_v.shape
    slot_dev, degs, nlat = legendre_ref.shape
    groups, lat_pairs = slot_dev // 2, lat_dev // 2
    rows = count * 8
    others = count - 1
    inv_root = 1.0 / math.sqrt(width)
    total_cells = float(lat_dev * count * width)

    barrier = pltpu.get_barrier_semaphore()

    def greet(step, carry):
        pl.semaphore_signal(barrier, inc=1, device_id={"lat": partner(me, step, count)}, device_id_type=MESH)
        return carry

    lax.fori_loop(1, count, greet, 0)
    loads = []
    for a in range(lat_dev):
        load = pltpu.make_async_copy(field_ref.at[a], field_v.at[a], field_sem.at[a])
        load.start()
        loads.append(load)
    mix_load = pltpu.make_async_copy(mixing_ref, mix_v, mix_sem)
    mix_load.start()

    columns = lax.broadcasted_iota(jnp.int32, (rows, 4 * pad), 1)
    for k in range(groups):
        select[k] = jnp.where(columns == target_ref[k], 1.0, 0.0).astype(BF16)

    squares = jnp.zeros((8, chans), F32)
    sums = jnp.zeros((1, chans), F32)
    for a in range(lat_dev):
        loads[a].wait()
        raw[a] = dot(table_ref[...], field_v[a])
        sums = sums + raw[a, 0:1, :]
        values = field_v[a].astype(F32)
        squares = squares + jnp.sum((values * values).reshape(width // 8, 8, chans), axis=0)
    square = jnp.sum(squares, axis=0, keepdims=True)
    own = jnp.concatenate([sums, square], axis=0)
    stat_src[...] = own
    stat_recv[pl.ds(me, 1)] = own[None]
    local_mean = sums / float(lat_dev * width)

    pl.semaphore_wait(barrier, others)

    def start_stat(step, carry):
        to = partner(me, count - step, count)
        pltpu.make_async_remote_copy(
            src_ref=stat_src, dst_ref=stat_recv.at[me], send_sem=stat_sems.at[0], recv_sem=stat_sems.at[1],
            device_id={"lat": to}, device_id_type=MESH,
        ).start()
        return carry

    lax.fori_loop(1, count, start_stat, 0)

    def start_group(k, source, target, sems):
        def body(step, carry):
            to = partner(me, count - step, count)
            pltpu.make_async_remote_copy(
                src_ref=source.at[k, to], dst_ref=target.at[k, me], send_sem=sems.at[0, k], recv_sem=sems.at[1, k],
                device_id={"lat": to}, device_id_type=MESH,
            ).start()
            return carry

        lax.fori_loop(1, count, body, 0)

    def wait_bytes(ref, sem):
        pltpu.make_async_copy(ref, ref, sem).wait()

    half = 2 * pad
    for p in range(lat_pairs):
        for parity in range(2):
            spec[p, parity * half : (parity + 1) * half, :] = (
                raw[2 * p + parity] - tsum_ref[...] * local_mean
            ).astype(BF16)
    for k in range(groups):
        for p in range(lat_pairs):
            picked = dot(select[k], spec[p])
            send[k, :, p] = picked.reshape(count, 8, chans).astype(BF16)
        recv[k, pl.ds(me, 1)] = send[k, pl.ds(me, 1)]
        start_group(k, send, recv, fwd_sems)

    col = lax.broadcasted_iota(jnp.int32, (nlat, 4 * nlat), 1)
    lat_row = lax.broadcasted_iota(jnp.int32, (nlat, 4 * nlat), 0)
    degree = lax.broadcasted_iota(jnp.int32, (degs, nlat), 0)
    for k in range(groups):
        for jj in range(2):
            slot = 2 * k + jj
            wave = wave_ref[me * slot_dev + slot]
            kept = jnp.where(degree >= wave, legendre_ref[slot].astype(F32), 0.0).astype(BF16)
            for r in range(2):
                q = 2 * jj + r
                spread = jnp.where(col == 4 * lat_row + q, 1.0, 0.0).astype(BF16)
                lbig[k, q * degs : (q + 1) * degs, :] = dot(kept, spread).astype(BF16)

    wait_bytes(stat_recv.at[pl.ds(0, others)], stat_sems.at[1])
    stats = stat_recv[...]
    total = jnp.sum(stats, axis=0)
    mean = total[0:1] / total_cells
    var = total[1:2] / total_cells - mean * mean
    scale = gain_ref[...] / jnp.sqrt(var + 1e-05)
    stat_ref[0:1] = mean
    stat_ref[1:2] = scale
    shift = (stats[:, 0, :] / float(lat_dev * width) - mean).astype(BF16)
    owner = lax.broadcasted_iota(jnp.int32, (4 * nlat, count), 1)
    lat_of = lax.broadcasted_iota(jnp.int32, (4 * nlat, count), 0)
    owned = jnp.where((lat_of >= owner * (4 * lat_dev)) & (lat_of < (owner + 1) * (4 * lat_dev)), 1.0, 0.0).astype(BF16)
    shift_lat = dot(owned, shift).astype(BF16)
    mode_scale = scale * inv_root
    lanes = lax.broadcasted_iota(jnp.int32, (1, 2 * pad), 1)
    mix_load.wait()

    for k in range(groups):
        wait_bytes(recv.at[k, pl.ds(0, others)], fwd_sems.at[1, k])
        arrived = recv[k].astype(F32).reshape(count * lat_pairs * 8, chans).astype(BF16)
        coef = dot(lbig[k], arrived)
        offset = dot(lbig[k], shift_lat)
        mixed = []
        for jj in range(2):
            slot = 2 * k + jj
            wave = wave_ref[me * slot_dev + slot]
            parts = []
            for r in range(2):
                q = slice((2 * jj + r) * degs, (2 * jj + r + 1) * degs)
                tsum = jnp.sum(jnp.where(lanes == wave + r * pad, tsum_row_ref[...], 0.0), axis=1, keepdims=True)
                parts.append(((coef[q] + tsum * offset[q]) * mode_scale).astype(BF16))
            both = jnp.concatenate(parts, axis=0)
            by_real = dot(both, mix_v[slot, 0])
            by_imag = dot(both, mix_v[slot, 1])
            weight = jnp.where(wave == 0, 1.0, 2.0) * math.sqrt(nlat / degs)
            mixed.append(((by_real[:degs] - by_imag[degs:]) * weight).astype(BF16))
            mixed.append(((by_imag[:degs] + by_real[degs:]) * weight).astype(BF16))
        mixed = jnp.concatenate(mixed, axis=0)
        back = lax.dot_general(lbig[k], mixed, (((0,), (0,)), ((), ())), preferred_element_type=F32)
        back_send[k] = back.reshape(count, lat_pairs, 8, chans).astype(BF16)
        ret_ref[k, pl.ds(me, 1)] = back_send[k, pl.ds(me, 1)]
        start_group(k, back_send, ret_ref, back_sems)

    wait_bytes(stat_recv.at[pl.ds(0, others)], stat_sems.at[0])
    for k in range(groups):
        wait_bytes(send.at[k, pl.ds(0, others)], fwd_sems.at[0, k])
    for k in range(groups):
        wait_bytes(ret_ref.at[k, pl.ds(0, others)], back_sems.at[1, k])
        wait_bytes(back_send.at[k, pl.ds(0, others)], back_sems.at[0, k])


def inverse_kernel(pad, ret_ref, target_ref, stat_ref, table_ref, field_ref, out_ref):
    groups, count, lat_pairs, _, chans = ret_ref.shape
    width = field_ref.shape[1]
    inv_root = 1.0 / math.sqrt(width)
    a = pl.program_id(0)
    pair, parity = a // 2, lax.rem(a, 2)
    rows = count * 8
    line = lax.broadcasted_iota(jnp.int32, (2 * pad, rows), 0) + parity * (2 * pad)
    waves = jnp.zeros((2 * pad, chans), F32)
    for k in range(groups):
        block = ret_ref[k, :, pl.ds(pair, 1)].astype(F32).reshape(rows, chans).astype(BF16)
        waves = waves + dot(jnp.where(line == target_ref[k], 1.0, 0.0).astype(BF16), block)
    filtered = dot(table_ref[...], waves.astype(BF16)) * inv_root
    normed = ((field_ref[0].astype(F32) - stat_ref[0:1]) * stat_ref[1:2]).astype(BF16)
    out_ref[0] = (normed.astype(F32) + filtered).astype(BF16)


def per_device(field, gain, slot_wave, legendre, mixing):
    count = lax.axis_size("lat")
    lat_dev, width, chans = field.shape
    slot_dev, degs, nlat = legendre.shape
    groups, lat_pairs = slot_dev // 2, lat_dev // 2
    table, pad = wave_table(degs, width)
    tsum = table.astype(np.float64).sum(axis=1).astype(np.float32)
    rows = count * 8
    waves = slot_wave.reshape(count, groups, 1, 2, 1).transpose(1, 0, 2, 3, 4)
    offsets = (np.arange(2).reshape(2, 1, 1) * 2 + np.arange(2).reshape(1, 1, 2)) * pad
    target = (waves + jnp.asarray(offsets, jnp.int32)).reshape(groups, rows)

    vmem = pl.BlockSpec(memory_space=pltpu.VMEM)
    anywhere = pl.BlockSpec(memory_space=pl.ANY)
    dma = pltpu.SemaphoreType.DMA
    block = (groups, count, lat_pairs, 8, chans)
    ret, stat = pl.pallas_call(
        functools.partial(exchange_kernel, count, pad),
        out_shape=(jax.ShapeDtypeStruct(block, BF16), jax.ShapeDtypeStruct((2, chans), F32)),
        in_specs=[anywhere, pl.BlockSpec(memory_space=pltpu.SMEM), vmem, vmem, vmem, vmem, vmem, vmem, anywhere],
        out_specs=(vmem, vmem),
        scratch_shapes=[
            pltpu.VMEM(field.shape, BF16),
            pltpu.VMEM(mixing.shape, BF16),
            pltpu.VMEM((groups, rows, 4 * pad), BF16),
            pltpu.VMEM((lat_dev, 2 * pad, chans), F32),
            pltpu.VMEM((lat_pairs, 4 * pad, chans), BF16),
            pltpu.VMEM(block, BF16),
            pltpu.VMEM(block, BF16),
            pltpu.VMEM(block, BF16),
            pltpu.VMEM((2, chans), F32),
            pltpu.VMEM((count, 2, chans), F32),
            pltpu.VMEM((groups, 4 * degs, 4 * nlat), BF16),
            dma((lat_dev,)),
            dma(()),
            dma((2,)),
            dma((2, groups)),
            dma((2, groups)),
        ],
        compiler_params=pltpu.CompilerParams(
            collective_id=0, has_side_effects=True, vmem_limit_bytes=60 * 2**20
        ),
        name="exchange",
    )(
        field, slot_wave, target.reshape(groups, rows, 1), gain.reshape(1, chans), jnp.asarray(table),
        jnp.asarray(tsum.reshape(-1, 1)), jnp.asarray(tsum.reshape(1, -1)), legendre, mixing,
    )
    whole = lambda shape: pl.BlockSpec(shape, lambda a: (0,) * len(shape))
    row_block = pl.BlockSpec((1, width, chans), lambda a: (a, 0, 0))
    return pl.pallas_call(
        functools.partial(inverse_kernel, pad),
        grid=(lat_dev,),
        out_shape=jax.ShapeDtypeStruct(field.shape, BF16),
        in_specs=[whole(block), whole((groups, 1, rows)), whole((2, chans)), whole((width, 2 * pad)), row_block],
        out_specs=row_block,
        compiler_params=pltpu.CompilerParams(vmem_limit_bytes=48 * 2**20),
        name="inverse",
    )(ret, target.reshape(groups, 1, rows), stat, jnp.asarray(table.T.copy()), field)


def solution(mesh):
    return jax.shard_map(
        per_device,
        mesh=mesh,
        in_specs=(
            P(("member", "lat"), None, None),
            P(),
            P(),
            P("lat", None, None),
            P("lat", None, None, None),
        ),
        out_specs=P(("member", "lat"), None, None),
        check_vma=False,
    )
```

time: 104 us -> 52.7 us (0.51)
  Pallas kernels: 0 us -> 45.5 us
  blocking collectives: 35 us -> 0 us
  waiting for transfers between devices: 33 us -> 0 us
  matrix products: 12.6 us -> 0 us
  starting transfers between devices: 8.95 us -> 0 us
  other arithmetic: 9.31 us -> 0.77 us
  local copies, waits for them, and re-layouts: 4.87 us -> 6.12 us
    pallas_call x0 -> x2, Pallas kernels: none -> 45.5 us  [the longest x1 39.7 us: per_device(): pl.pallas_call(functools.partial(exchange_kernel, count, pad), out_shape=...]
    psum x1 -> x0, blocking collectives: 35 us -> none  [per_device(): total, squares = lax.psum((local_sum, local_sq), 'lat')]
    all_to_all x2 -> x0, waiting for transfers between devices: 33 us -> none  [the longest x1 17.2 us: per_device(): lax.all_to_all(spectrum, 'lat', split_axis=0, concat_axis=1, tiled=True)[0]]
    dot_general x4 -> x0, matrix products: 12.6 us -> none  [the longest x1 6.16 us: per_device(): jnp.einsum('akrc,rkn->anc', returned, inverse, preferred_element_type=jnp...]
    all_to_all x2 -> x0, starting transfers between devices: 8.95 us -> none  [the longest x1 5.33 us: per_device(): lax.all_to_all(back, 'lat', split_axis=0, concat_axis=2, tiled=True)[0]]
    another operation x2 -> x0, other arithmetic: 5.69 us -> none
    unnamed x8, local copies, waits for them, and re-layouts: 0.02 us -> 3.98 us
    reduce_sum x1 -> x0, other arithmetic: 3.47 us -> none  [per_device(): local_sum = jnp.sum(values, axis=(0, 1))]
  transfers between devices with their start and end apart: 2 -> 0, of which waited for: 2 -> 0; matrix products, arithmetic and copies ran while one was open for 4% -> 0% of each run, Pallas kernels for 0% -> 0%
where the time goes in v1:
time: 52.7 us; the launch traced here: 52.4 us
  Pallas kernels  45.5 us (86%)
  local copies, waits for them, and re-layouts  6.12 us (12%)
  other arithmetic  0.77 us (1%)
    pallas_call x1, Pallas kernels, per_device(): pl.pallas_call(functools.partial(exchange_kernel, count, pad), out_shape=...  39.7 us
    pallas_call x1, Pallas kernels, per_device(): pl.pallas_call(functools.partial(inverse_kernel, pad), grid=(lat_dev,), o...  5.72 us
    unnamed x8, local copies, waits for them, and re-layouts  3.98 us
    add x6, local copies, waits for them, and re-layouts, per_device(): target = (waves + jnp.asarray(offsets, jnp.int32)).reshape(groups, rows)  1.35 us

profile of v1, /device:TPU:0, one launch (start us, length us, event | category | flops | bytes accessed | tf_op | source)
XLA Modules:
  0.0 52.4 jit_solution(3845624100167045740)
XLA Ops:
  0.0 0.0 copy-start.1
  0.0 0.8 %add.47 = s32[16,2,2,2]{3,2,1,0:T(2,128)S(1)} broadcast(s32[2,2]{1,0:T(2,128)} %constant.18), dimensions={1,3} | broadcast | bytes 528 | tf_op jit(solution)/shard_map/add | solution.py:223
  0.8 0.1 add.48
  0.9 0.8 %reshape.75 = s32[16,3,1,2,1]{3,1,0,4,2:T(4,128)S(1)} reshape(s32[96]{0:T(128)} %wave_ref.1) | data formatting | bytes 768 | tf_op jit(solution)/shard_map/reshape | solution.py:221
  1.7 0.1 add.44
  1.8 0.2 add.55
  2.0 0.2 add.54
  2.2 0.8 %broadcast_add_fusion.target_ref = s32[3,128,1]{2,1,0:T(8,128)} fusion(s32[3,128,1]{2,1,0:T(8,128)S(1)} %add.54, s32[128]{0:T(128)S(1)} %add.48), kind=kLoop, calls=%fused_computation | loop fusion | flops 384 | bytes 3584 | tf_op jit(solution)/shard_map/add | solution.py:223
  2.9 39.7 %exchange.1 = (bf16[3,16,3,8,256]{4,3,2,1,0:T(8,128)(2,1)}, f32[2,256]{1,0:T(2,128)}) custom-call(bf16[6,1440,256]{2,1,0:T(8,128)(2,1)} %field_ref.3, s32[96]{0:T(128)} %wave_ref.1, s32[3,128,1]{2,1,0:T(8,128)} %broadcast_add_fusion.target_ref, f32[1,256]{1,0:T(1,128)} %bitcast.5, bf16[256,1440]{1,0:T(8,128)(2,1)} %constant.11.clone.table_ref, ...), custom_call_target="tpu_custom_call" | custom-call | tf_op jit(solution)/shard_map/exchange/pallas_call | solution.py:229
  42.7 0.0 copy-done.1
  42.7 0.0 copy-start
  42.7 2.2 %copy-done = bf16[6,1440,256]{2,1,0:T(8,128)(2,1)S(1)} copy-done((bf16[6,1440,256]{2,1,0:T(8,128)(2,1)S(1)}, bf16[6,1440,256]{2,1,0:T(8,128)(2,1)}, u32[]{:S(2)}) %copy-start) | copy-done | bytes 4423704
  44.9 0.0 copy-start.2
  44.9 1.1 %copy-done.2 = bf16[3,16,3,8,256]{4,3,2,1,0:T(8,128)(2,1)S(1)} copy-done((bf16[3,16,3,8,256]{4,3,2,1,0:T(8,128)(2,1)S(1)}, bf16[3,16,3,8,256]{4,3,2,1,0:T(8,128)(2,1)}, u32[]{:S(2)}) %copy-start.2) | copy-done | bytes 589848
  46.0 0.0 copy-start.3
  46.0 0.7 %copy-done.3 = f32[2,256]{1,0:T(2,128)S(1)} copy-done((f32[2,256]{1,0:T(2,128)S(1)}, f32[2,256]{1,0:T(2,128)}, u32[]{:S(2)}) %copy-start.3) | copy-done | bytes 2072
  46.7 5.7 %inverse.1 = bf16[6,1440,256]{2,1,0:T(8,128)(2,1)} custom-call(bf16[3,16,3,8,256]{4,3,2,1,0:T(8,128)(2,1)S(1)} %copy-done.2, s32[3,1,128]{2,1,0:T(1,128)S(1)} %broadcast_add_fusion.1.target_ref, f32[2,256]{1,0:T(2,128)S(1)} %copy-done.3, bf16[1440,256]{1,0:T(8,128)(2,1)S(1)} %copy-done.1, bf16[6,1440,256]{2,1,0:T(8,128)(2,1)S(1)} %copy-done), custom_call_target="tpu_custom_call" | custom-call | tf_op jit(solution)/shard_map/inverse/pallas_call | solution.py:262
  (2 shorter events, 0.0 us)
Async XLA Ops:
  0.0 42.7 %copy-start.1 = (bf16[1440,256]{1,0:T(8,128)(2,1)S(1)}, bf16[1440,256]{1,0:T(8,128)(2,1)}, u32[]{:S(2)}) copy-start(bf16[1440,256]{1,0:T(8,128)(2,1)} %constant.14.clone.table_ref) | copy-start | bytes 2211844
  42.7 2.3 %copy-start = (bf16[6,1440,256]{2,1,0:T(8,128)(2,1)S(1)}, bf16[6,1440,256]{2,1,0:T(8,128)(2,1)}, u32[]{:S(2)}) copy-start(bf16[6,1440,256]{2,1,0:T(8,128)(2,1)} %field_ref.3) | copy-start | bytes 13271044
  44.9 1.1 %copy-start.2 = (bf16[3,16,3,8,256]{4,3,2,1,0:T(8,128)(2,1)S(1)}, bf16[3,16,3,8,256]{4,3,2,1,0:T(8,128)(2,1)}, u32[]{:S(2)}) copy-start(bf16[3,16,3,8,256]{4,3,2,1,0:T(8,128)(2,1)} %get-tuple-element.7.ret_ref) | copy-start | bytes 1769476
  46.0 0.7 %copy-start.3 = (f32[2,256]{1,0:T(2,128)S(1)}, f32[2,256]{1,0:T(2,128)}, u32[]{:S(2)}) copy-start(f32[2,256]{1,0:T(2,128)} %get-tuple-element.8.stat_ref) | copy-start | bytes 6148

commit v2 on v1

--- a/solution.py
+++ b/solution.py
@@ -43,10 +43,11 @@
 def exchange_kernel(
     count,
     pad,
-    field_ref, wave_ref, target_ref, gain_ref, table_ref, tsum_ref, tsum_row_ref, legendre_ref, mixing_ref,
-    ret_ref, stat_ref,
-    field_v, mix_v, select, raw, spec, send, recv, back_send, stat_src, stat_recv, lbig,
-    field_sem, mix_sem, stat_sems, fwd_sems, back_sems,
+    field_ref, wave_hbm, wave_row_hbm, gain_hbm, table_hbm, tsum_hbm, legendre_hbm, mixing_hbm,
+    ret_ref, target_ref, field_v,
+    wave_ref, wave_row_ref, gain_ref, table_ref, tsum_row_ref, legendre_ref, mix_v,
+    select, raw, spec, send, recv, back_send, stat_src, stat_recv, lbig,
+    field_sem, load_sem, stat_sems, fwd_sems, back_sems,
 ):
     me = lax.axis_index("lat")
     lat_dev, width, chans = field_v.shape
@@ -63,19 +64,44 @@
         pl.semaphore_signal(barrier, inc=1, device_id={"lat": partner(me, step, count)}, device_id_type=MESH)
         return carry
 
-    lax.fori_loop(1, count, greet, 0)
+    def load_of(index, source, target):
+        load = pltpu.make_async_copy(source, target, load_sem.at[index])
+        load.start()
+        return load
+
+    row_load = load_of(0, wave_row_hbm, wave_row_ref)
+    table_load = load_of(1, table_hbm, table_ref)
+    tsum_load = load_of(2, tsum_hbm, tsum_row_ref)
     loads = []
     for a in range(lat_dev):
         load = pltpu.make_async_copy(field_ref.at[a], field_v.at[a], field_sem.at[a])
         load.start()
         loads.append(load)
-    mix_load = pltpu.make_async_copy(mixing_ref, mix_v, mix_sem)
-    mix_load.start()
-
-    columns = lax.broadcasted_iota(jnp.int32, (rows, 4 * pad), 1)
-    for k in range(groups):
-        select[k] = jnp.where(columns == target_ref[k], 1.0, 0.0).astype(BF16)
-
+    late = [
+        load_of(3, wave_hbm, wave_ref),
+        load_of(4, legendre_hbm, legendre_ref),
+        load_of(5, gain_hbm, gain_ref),
+        load_of(6, mixing_hbm, mix_v),
+    ]
+    lax.fori_loop(1, count, greet, 0)
+
+    slots = count * slot_dev
+    row_load.wait()
+    wave_row = wave_row_ref[...].astype(F32)
+    columns = lax.broadcasted_iota(jnp.int32, (rows, 4 * pad), 1).astype(F32)
+    row = lax.broadcasted_iota(jnp.int32, (rows, 1), 0)
+    slot_lane = lax.broadcasted_iota(jnp.int32, (rows, slots), 1)
+    for k in range(groups):
+        slot_of = row // 8 * slot_dev + 2 * k + row % 4 // 2
+        wave_of = jnp.sum(jnp.where(slot_lane == slot_of, wave_row, 0.0), axis=1, keepdims=True)
+        target = wave_of + ((row % 8 // 4 * 2 + row % 2) * pad).astype(F32)
+        select[k] = jnp.where(columns == target, 1.0, 0.0).astype(BF16)
+
+    tsum_load.wait()
+    part_a = lax.broadcasted_iota(jnp.int32, (2 * pad, 2 * pad), 0)
+    part_b = lax.broadcasted_iota(jnp.int32, (2 * pad, 2 * pad), 1)
+    tsum_col = jnp.sum(jnp.where(part_a == part_b, tsum_row_ref[...], 0.0), axis=1, keepdims=True)
+    table_load.wait()
     squares = jnp.zeros((8, chans), F32)
     sums = jnp.zeros((1, chans), F32)
     for a in range(lat_dev):
@@ -120,7 +146,7 @@
     for p in range(lat_pairs):
         for parity in range(2):
             spec[p, parity * half : (parity + 1) * half, :] = (
-                raw[2 * p + parity] - tsum_ref[...] * local_mean
+                raw[2 * p + parity] - tsum_col * local_mean
             ).astype(BF16)
     for k in range(groups):
         for p in range(lat_pairs):
@@ -128,6 +154,18 @@
             send[k, :, p] = picked.reshape(count, 8, chans).astype(BF16)
         recv[k, pl.ds(me, 1)] = send[k, pl.ds(me, 1)]
         start_group(k, send, recv, fwd_sems)
+
+    for load in late:
+        load.wait()
+    slot_a = lax.broadcasted_iota(jnp.int32, (slots, slots), 0)
+    slot_b = lax.broadcasted_iota(jnp.int32, (slots, slots), 1)
+    wave_col = jnp.sum(jnp.where(slot_a == slot_b, wave_row, 0.0), axis=1, keepdims=True)
+    lane = lax.broadcasted_iota(jnp.int32, (1, rows), 1)
+    slot_line = lax.broadcasted_iota(jnp.int32, (slots, rows), 0)
+    for k in range(groups):
+        slot_of = lane // 8 * slot_dev + 2 * k + lane % 4 // 2
+        wave_of = jnp.sum(jnp.where(slot_line == slot_of, wave_col, 0.0), axis=0, keepdims=True)
+        target_ref[:, k * rows : (k + 1) * rows] = wave_of + ((lane % 8 // 4 * 2 + lane % 2) * pad).astype(F32)
 
     col = lax.broadcasted_iota(jnp.int32, (nlat, 4 * nlat), 1)
     lat_row = lax.broadcasted_iota(jnp.int32, (nlat, 4 * nlat), 0)
@@ -148,8 +186,6 @@
     mean = total[0:1] / total_cells
     var = total[1:2] / total_cells - mean * mean
     scale = gain_ref[...] / jnp.sqrt(var + 1e-05)
-    stat_ref[0:1] = mean
-    stat_ref[1:2] = scale
     shift = (stats[:, 0, :] / float(lat_dev * width) - mean).astype(BF16)
     owner = lax.broadcasted_iota(jnp.int32, (4 * nlat, count), 1)
     lat_of = lax.broadcasted_iota(jnp.int32, (4 * nlat, count), 0)
@@ -157,9 +193,14 @@
     shift_lat = dot(owned, shift).astype(BF16)
     mode_scale = scale * inv_root
     lanes = lax.broadcasted_iota(jnp.int32, (1, 2 * pad), 1)
-    mix_load.wait()
-
-    for k in range(groups):
+
+    def normalize(a):
+        field_v[a] = ((field_v[a].astype(F32) - mean) * scale).astype(BF16)
+
+    for k in range(groups):
+        if k > 0:
+            for a in range((k - 1) * lat_dev // groups, k * lat_dev // groups):
+                normalize(a)
         wait_bytes(recv.at[k, pl.ds(0, others)], fwd_sems.at[1, k])
         arrived = recv[k].astype(F32).reshape(count * lat_pairs * 8, chans).astype(BF16)
         coef = dot(lbig[k], arrived)
@@ -176,7 +217,7 @@
             both = jnp.concatenate(parts, axis=0)
             by_real = dot(both, mix_v[slot, 0])
             by_imag = dot(both, mix_v[slot, 1])
-            weight = jnp.where(wave == 0, 1.0, 2.0) * math.sqrt(nlat / degs)
+            weight = jnp.where(wave == 0, 1.0, 2.0) * (math.sqrt(nlat / degs) * inv_root)
             mixed.append(((by_real[:degs] - by_imag[degs:]) * weight).astype(BF16))
             mixed.append(((by_imag[:degs] + by_real[degs:]) * weight).astype(BF16))
         mixed = jnp.concatenate(mixed, axis=0)
@@ -185,6 +226,8 @@
         ret_ref[k, pl.ds(me, 1)] = back_send[k, pl.ds(me, 1)]
         start_group(k, back_send, ret_ref, back_sems)
 
+    for a in range((groups - 1) * lat_dev // groups, lat_dev):
+        normalize(a)
     wait_bytes(stat_recv.at[pl.ds(0, others)], stat_sems.at[0])
     for k in range(groups):
         wait_bytes(send.at[k, pl.ds(0, others)], fwd_sems.at[0, k])
@@ -193,21 +236,16 @@
         wait_bytes(back_send.at[k, pl.ds(0, others)], back_sems.at[0, k])
 
 
-def inverse_kernel(pad, ret_ref, target_ref, stat_ref, table_ref, field_ref, out_ref):
+def inverse_kernel(pad, ret_ref, target_ref, table_ref, normed_ref, out_ref):
     groups, count, lat_pairs, _, chans = ret_ref.shape
-    width = field_ref.shape[1]
-    inv_root = 1.0 / math.sqrt(width)
     a = pl.program_id(0)
     pair, parity = a // 2, lax.rem(a, 2)
-    rows = count * 8
-    line = lax.broadcasted_iota(jnp.int32, (2 * pad, rows), 0) + parity * (2 * pad)
-    waves = jnp.zeros((2 * pad, chans), F32)
-    for k in range(groups):
-        block = ret_ref[k, :, pl.ds(pair, 1)].astype(F32).reshape(rows, chans).astype(BF16)
-        waves = waves + dot(jnp.where(line == target_ref[k], 1.0, 0.0).astype(BF16), block)
-    filtered = dot(table_ref[...], waves.astype(BF16)) * inv_root
-    normed = ((field_ref[0].astype(F32) - stat_ref[0:1]) * stat_ref[1:2]).astype(BF16)
-    out_ref[0] = (normed.astype(F32) + filtered).astype(BF16)
+    rows = groups * count * 8
+    line = (lax.broadcasted_iota(jnp.int32, (2 * pad, rows), 0) + parity * (2 * pad)).astype(F32)
+    place = jnp.where(line == target_ref[...], 1.0, 0.0).astype(BF16)
+    block = ret_ref[:, :, pl.ds(pair, 1)].astype(F32).reshape(rows, chans).astype(BF16)
+    filtered = dot(table_ref[...], dot(place, block).astype(BF16))
+    out_ref[0] = (normed_ref[a].astype(F32) + filtered).astype(BF16)
 
 
 def per_device(field, gain, slot_wave, legendre, mixing):
@@ -218,21 +256,27 @@
     table, pad = wave_table(degs, width)
     tsum = table.astype(np.float64).sum(axis=1).astype(np.float32)
     rows = count * 8
-    waves = slot_wave.reshape(count, groups, 1, 2, 1).transpose(1, 0, 2, 3, 4)
-    offsets = (np.arange(2).reshape(2, 1, 1) * 2 + np.arange(2).reshape(1, 1, 2)) * pad
-    target = (waves + jnp.asarray(offsets, jnp.int32)).reshape(groups, rows)
-
     vmem = pl.BlockSpec(memory_space=pltpu.VMEM)
-    anywhere = pl.BlockSpec(memory_space=pl.ANY)
+    hbm = pl.BlockSpec(memory_space=pltpu.HBM)
     dma = pltpu.SemaphoreType.DMA
+    half_limit = 30 * 2**20
     block = (groups, count, lat_pairs, 8, chans)
-    ret, stat = pl.pallas_call(
+    ret, target, normed = pl.pallas_call(
         functools.partial(exchange_kernel, count, pad),
-        out_shape=(jax.ShapeDtypeStruct(block, BF16), jax.ShapeDtypeStruct((2, chans), F32)),
-        in_specs=[anywhere, pl.BlockSpec(memory_space=pltpu.SMEM), vmem, vmem, vmem, vmem, vmem, vmem, anywhere],
-        out_specs=(vmem, vmem),
+        out_shape=(
+            jax.ShapeDtypeStruct(block, BF16),
+            jax.ShapeDtypeStruct((1, groups * rows), F32),
+            jax.ShapeDtypeStruct(field.shape, BF16),
+        ),
+        in_specs=[hbm] * 8,
+        out_specs=(vmem, vmem, vmem),
         scratch_shapes=[
-            pltpu.VMEM(field.shape, BF16),
+            pltpu.SMEM(slot_wave.shape, jnp.int32),
+            pltpu.VMEM((1,) + slot_wave.shape, jnp.int32),
+            pltpu.VMEM((1, chans), F32),
+            pltpu.VMEM(table.shape, BF16),
+            pltpu.VMEM((1, 2 * pad), F32),
+            pltpu.VMEM(legendre.shape, BF16),
             pltpu.VMEM(mixing.shape, BF16),
             pltpu.VMEM((groups, rows, 4 * pad), BF16),
             pltpu.VMEM((lat_dev, 2 * pad, chans), F32),
@@ -244,30 +288,28 @@
             pltpu.VMEM((count, 2, chans), F32),
             pltpu.VMEM((groups, 4 * degs, 4 * nlat), BF16),
             dma((lat_dev,)),
-            dma(()),
+            dma((7,)),
             dma((2,)),
             dma((2, groups)),
             dma((2, groups)),
         ],
         compiler_params=pltpu.CompilerParams(
-            collective_id=0, has_side_effects=True, vmem_limit_bytes=60 * 2**20
+            collective_id=0, has_side_effects=True, vmem_limit_bytes=half_limit if count <= 16 else 2 * half_limit
         ),
         name="exchange",
-    )(
-        field, slot_wave, target.reshape(groups, rows, 1), gain.reshape(1, chans), jnp.asarray(table),
-        jnp.asarray(tsum.reshape(-1, 1)), jnp.asarray(tsum.reshape(1, -1)), legendre, mixing,
-    )
-    whole = lambda shape: pl.BlockSpec(shape, lambda a: (0,) * len(shape))
-    row_block = pl.BlockSpec((1, width, chans), lambda a: (a, 0, 0))
+    )(*(pltpu.with_memory_space_constraint(x, pltpu.HBM) for x in (
+        field, slot_wave, slot_wave.reshape(1, -1), gain.reshape(1, chans), jnp.asarray(table),
+        jnp.asarray(tsum.reshape(1, -1)), legendre, mixing,
+    )))
     return pl.pallas_call(
         functools.partial(inverse_kernel, pad),
         grid=(lat_dev,),
         out_shape=jax.ShapeDtypeStruct(field.shape, BF16),
-        in_specs=[whole(block), whole((groups, 1, rows)), whole((2, chans)), whole((width, 2 * pad)), row_block],
-        out_specs=row_block,
-        compiler_params=pltpu.CompilerParams(vmem_limit_bytes=48 * 2**20),
+        in_specs=[vmem, vmem, vmem, vmem],
+        out_specs=pl.BlockSpec((1, width, chans), lambda a: (a, 0, 0)),
+        compiler_params=pltpu.CompilerParams(vmem_limit_bytes=half_limit),
         name="inverse",
-    )(ret, target.reshape(groups, 1, rows), stat, jnp.asarray(table.T.copy()), field)
+    )(ret, target, jnp.asarray(table.T.copy()), normed)
 
 
 def solution(mesh):

time: 52.7 us -> 42.5 us (0.81)
  local copies, waits for them, and re-layouts: 6.12 us -> 0.01 us
  Pallas kernels: 45.5 us -> 42.4 us
  other arithmetic: 0.77 us -> 0 us
    unnamed x8 -> x2, local copies, waits for them, and re-layouts: 3.98 us -> 0.01 us
    pallas_call x1, Pallas kernels: 39.7 us -> 37 us  [per_device(): pl.pallas_call(functools.partial(exchange_kernel, count, pad), out_shape=...]
    add x6 -> x0, local copies, waits for them, and re-layouts: 1.35 us -> none  [per_device(): target = (waves + jnp.asarray(offsets, jnp.int32)).reshape(groups, rows)]
    reshape x1 -> x0, local copies, waits for them, and re-layouts: 0.79 us -> none  [per_device(): waves = slot_wave.reshape(count, groups, 1, 2, 1).transpose(1, 0, 2, 3, 4)]
    add x2 -> x0, other arithmetic: 0.77 us -> none  [per_device(): target = (waves + jnp.asarray(offsets, jnp.int32)).reshape(groups, rows)]
where the time goes in v2:
time: 42.5 us; the launch traced here: 42.4 us
  Pallas kernels  42.4 us (100%)
    pallas_call x1, Pallas kernels, per_device(): pl.pallas_call(functools.partial(exchange_kernel, count, pad), out_shape=...  37 us
    pallas_call x1, Pallas kernels, per_device(): pl.pallas_call(functools.partial(inverse_kernel, pad), grid=(lat_dev,), o...  5.33 us

profile of v2, /device:TPU:0, one launch (start us, length us, event | category | flops | bytes accessed | tf_op | source)
XLA Modules:
  0.0 42.4 jit_solution(17879899608382737369)
XLA Ops:
  0.0 0.0 copy-start
  0.0 37.0 %exchange.1 = (bf16[3,16,3,8,256]{4,3,2,1,0:T(8,128)(2,1)S(1)}, f32[1,384]{1,0:T(1,128)S(1)}, bf16[6,1440,256]{2,1,0:T(8,128)(2,1)S(1)}) custom-call(bf16[6,1440,256]{2,1,0:T(8,128)(2,1)} %field_ref.1, s32[96]{0:T(128)} %wave_hbm.1, s32[1,96]{1,0:T(1,128)} %bitcast.2, f32[1,256]{1,0:T(1,128)} %bitcast.3, bf16[256,1440]{1,0:T(8,128)(2,1)} %constant.6.clone.table_hbm, ...), custom_call_target="tpu_custom_call" | custom-call | tf_op jit(solution)/shard_map/exchange/pallas_call | solution.py:264
  37.1 0.0 copy-done
  37.1 5.3 %inverse.1 = bf16[6,1440,256]{2,1,0:T(8,128)(2,1)} custom-call(bf16[3,16,3,8,256]{4,3,2,1,0:T(8,128)(2,1)S(1)} %get-tuple-element.8.ret_ref, f32[1,384]{1,0:T(1,128)S(1)} %get-tuple-element.9.target_ref, bf16[1440,256]{1,0:T(8,128)(2,1)S(1)} %copy-done, bf16[6,1440,256]{2,1,0:T(8,128)(2,1)S(1)} %get-tuple-element.10.normed_ref), custom_call_target="tpu_custom_call" | custom-call | tf_op jit(solution)/shard_map/inverse/pallas_call | solution.py:304
Async XLA Ops:
  0.0 37.1 %copy-start = (bf16[1440,256]{1,0:T(8,128)(2,1)S(1)}, bf16[1440,256]{1,0:T(8,128)(2,1)}, u32[]{:S(2)}) copy-start(bf16[1440,256]{1,0:T(8,128)(2,1)} %constant.8.clone.table_ref) | copy-start | bytes 2211844
